TPU v7x, 32 devices: a whole 2x2x4 slice. The times are simulated.
32 devices in a mesh: space: 8 (over z, y), tm: 4 (over x, core).
Axes of the slice: x: 2, y: 2, z: 4, core: 2. Of those that a mesh axis runs over, the one named last changes fastest.
Arguments:
- innovations: bfloat16 [12, 32, 768, 1536], P('tm', None, 'space'), may hold values from -6 to 6
- obs_counts: int32 [12, 192, 384], P('tm', 'space'), may hold values from 0 to 3
- diffusion: float32 [32, 192, 384], P(None, 'space'), may hold values from 0.01 to 0.1
- courant: float32 [32, 192, 384], P(None, 'space'), may hold values from 0 to 0.4
Outputs:
- increment: float32 [32, 768, 1536], P('tm', 'space')
- residual: float32 [32, 192, 384], P('tm', 'space')
All inputs are finite; a program needn't handle non-finite values.
Results may differ from a plain program's by a relative error of at most 0.0003.
Values sent between devices are 32-bit elements; how exact they have to be, the bound alone decides.
A program may use at most 384 MiB of HBM per device.

v0:
```python
import jax
import jax.numpy as jnp
from jax import lax
from jax.sharding import PartitionSpec as P

ITERS = 3


def padded_2(cells, sides, width):
    for axis, dim in sides:
        count = lax.axis_size(axis)
        ends = count - 1
        head = lax.slice_in_dim(cells, 0, width, axis=dim)
        tail = lax.slice_in_dim(cells, cells.shape[dim] - width, cells.shape[dim], axis=dim)
        cells = jnp.concatenate(
            [
                lax.ppermute(tail, axis, [(i, (i + 1) % count) for i in range(ends)]),
                cells,
                lax.ppermute(head, axis, [((i + 1) % count, i) for i in range(ends)]),
            ],
            axis=dim,
        )
    return cells


def laplace_rows(padded, state_field):
    return (
        padded[:, 2:, :]
        + padded[:, :-2, :]
        + jnp.roll(state_field, 1, 2)
        + jnp.roll(state_field, -1, 2)
        - 4.0 * state_field
    )


def tangent(state_field, diffusion, courant):
    padded = padded_2(state_field, (("space", 1),), 1)
    return (
        state_field
        + diffusion * laplace_rows(padded, state_field)
        - courant * (state_field - jnp.roll(state_field, 1, 2))
    )


def adjoint(state_field, diffusion, courant):
    carried = courant * state_field
    spread = diffusion * state_field
    padded = padded_2(spread, (("space", 1),), 1)
    return state_field + laplace_rows(padded, spread) - carried + jnp.roll(carried, -1, 2)


def level_squares(residual):
    return lax.psum(jnp.sum(residual * residual), ("space", "tm"))


def level_curve(direction, hessian_image):
    return lax.psum(jnp.sum(direction * hessian_image), ("space", "tm"))


def solve_inner(rhs_field, hessian_part, norm_fn, curve_fn):
    control = jnp.zeros_like(rhs_field)
    residual = rhs_field
    direction = rhs_field
    norm_now = norm_fn(residual)
    for iter_no in range(ITERS):
        hessian_image = direction + hessian_part(direction)
        step_len = norm_now / curve_fn(direction, hessian_image)
        control = control + step_len * direction
        residual = residual - step_len * hessian_image
        if iter_no + 1 < ITERS:
            norm_next = norm_fn(residual)
            direction = residual + norm_next / norm_now * direction
            norm_now = norm_next
    return (control, residual)


def on_device(innovations, obs_counts, diffusion, courant):
    step_dev = obs_counts.shape[0]
    n_sections = lax.axis_size("tm")
    section_pos = lax.axis_index("tm")
    total_steps = step_dev * n_sections
    weights = obs_counts.astype(jnp.float32)[:, None]
    levels, fine_rows, fine_cols = (
        innovations.shape[1],
        innovations.shape[2],
        innovations.shape[3],
    )
    lev_part = levels // n_sections
    blocks = innovations.reshape(step_dev, levels, fine_rows // 4, 4, fine_cols // 4, 4).astype(
        jnp.float32
    )
    forcing = weights * jnp.mean(blocks, axis=(3, 5))
    all_weights = lax.all_gather(obs_counts, "tm", axis=0, tiled=True).astype(jnp.float32)[:, None]
    all_forcing = lax.all_to_all(forcing, "tm", split_axis=1, concat_axis=0, tiled=True)
    diff_part = lax.dynamic_slice_in_dim(diffusion, section_pos * lev_part, lev_part, 0)
    cour_part = lax.dynamic_slice_in_dim(courant, section_pos * lev_part, lev_part, 0)

    def level_back(terms):
        current = terms[total_steps - 1]
        for step_no in range(total_steps - 2, -1, -1):
            current = terms[step_no] + adjoint(current, diff_part, cour_part)
        return current

    def level_hess(state_field):
        records = []
        for step_no in range(total_steps):
            records.append(all_weights[step_no] * state_field)
            if step_no + 1 < total_steps:
                state_field = tangent(state_field, diff_part, cour_part)
        return level_back(jnp.stack(records))

    control, residual = solve_inner(level_back(all_forcing), level_hess, level_squares, level_curve)
    increment = jnp.repeat(jnp.repeat(control, 4, axis=1), 4, axis=2)
    return (increment, residual)


def solution(mesh):
    placed = (
        P("tm", None, "space", None),
        P("tm", "space", None),
        P(None, "space", None),
        P(None, "space", None),
    )
    return jax.shard_map(
        on_device,
        mesh=mesh,
        in_specs=placed,
        out_specs=(P("tm", "space", None), P("tm", "space", None)),
        check_vma=False,
    )
```

profile of v0, /device:TPU:0, one launch (start us, length us, event | category | flops | bytes accessed | tf_op | source)
XLA Modules:
  0.0 1311.0 jit_solution(5133714169819130187)
XLA Ops:
  0.6 115.2 %copy.14 = f32[3,32,96,1536]{1,3,2,0:T(8,128)} copy(bf16[3,32,96,1536]{3,2,1,0:T(8,128)(2,1)} %param.4) | data formatting | bytes 84934656 | tf_op jit(solution)/shard_map/convert_element_type | solution.py:89
  115.9 155.1 %reduce_sum.63 = f32[3,32,24,384]{1,3,2,0:T(8,128)} reduce(f32[3,32,24,4,384,4]{1,5,4,3,2,0:T(4,128)} %bitcast, f32[]{:T(128)} %constant.7.clone.1), dimensions={3,5}, to_apply=%region_0.0 | reduce | flops 13271040 | bytes 60162052 | tf_op jit(solution)/shard_map/reduce_sum | solution.py:92
  271.0 12.6 broadcast_multiply_fusion
  283.6 11.0 copy.15
  299.3 44.9 %all_gather.3 = s32[12,24,384]{2,1,0:T(8,128)S(1)} all-gather(s32[3,24,384]{2,1,0:T(8,128)S(1)} %copy-done.31), channel_id=1, replica_groups=mesh['space'=8,'tm'=4] {'tm'}, dimensions={0}, use_global_device_ids=true | all-gather | bytes 552960 | tf_op jit(solution)/shard_map/all_gather | solution.py:93
  368.4 5.7 collective-permute-start.5
  455.9 6.2 collective-permute-start.21
  495.3 5.8 collective-permute-start.29
  524.9 5.7 collective-permute-start.35
  554.5 5.7 collective-permute-start.41
  582.1 5.7 collective-permute-start.47
  608.9 5.7 collective-permute-start.53
  644.6 5.9 collective-permute-start.61
  670.5 44.6 %all-reduce = (f32[]{:T(128)}, f32[]{:T(128)}) all-reduce(f32[]{:T(128)} %get-tuple-element.9, f32[]{:T(128)} %get-tuple-element.8), channel_id=1, replica_groups=mesh['space'=8,'tm'=4] {'space','tm'}, use_global_device_ids=true, to_apply=%region_2.3 | all-reduce | flops 2 | bytes 16 | tf_op jit(solution)/shard_map/psum | solution.py:53
  717.1 41.6 %psum.44 = f32[]{:T(128)} all-reduce(f32[]{:T(128)} %multiply_reduce_fusion.3), channel_id=1, replica_groups=mesh['space'=8,'tm'=4] {'space','tm'}, use_global_device_ids=true, to_apply=%region_6.7 | all-reduce | flops 1 | bytes 8 | tf_op jit(solution)/shard_map/psum | solution.py:53
  795.9 5.7 collective-permute-start.75
  893.3 5.9 collective-permute-start.97
  937.9 5.8 collective-permute-start.107
  955.7 44.5 %psum.45 = f32[]{:T(128)} all-reduce(f32[]{:T(128)} %get-tuple-element.38), channel_id=1, replica_groups=mesh['space'=8,'tm'=4] {'space','tm'}, use_global_device_ids=true, to_apply=%region_8.9 | all-reduce | flops 1 | bytes 8 | tf_op jit(solution)/shard_map/psum | solution.py:57
  1003.3 41.6 %psum.46 = f32[]{:T(128)} all-reduce(f32[]{:T(128)} %get-tuple-element.36), channel_id=1, replica_groups=mesh['space'=8,'tm'=4] {'space','tm'}, use_global_device_ids=true, to_apply=%region_10.11 | all-reduce | flops 1 | bytes 8 | tf_op jit(solution)/shard_map/psum | solution.py:53
  1154.2 6.0 collective-permute-start.133
  1234.6 5.8 collective-permute-start.151
  1251.7 44.6 %psum.47 = f32[]{:T(128)} all-reduce(f32[]{:T(128)} %get-tuple-element.12), channel_id=1, replica_groups=mesh['space'=8,'tm'=4] {'space','tm'}, use_global_device_ids=true, to_apply=%region_12.13 | all-reduce | flops 1 | bytes 8 | tf_op jit(solution)/shard_map/psum | solution.py:57
  1304.5 6.1 copy.20
  (814 shorter events, 660.8 us)
Async XLA Ops:
  294.6 49.9 %all-to-all-start = ((f32[3,32,24,384]{3,2,0,1:T(8,128)}), f32[3,32,24,384]{3,2,0,1:T(8,128)}, u32[]{:S(2)}, u32[]{:S(2)}) async-start(f32[3,32,24,384]{3,2,0,1:T(8,128)} %copy.15), calls=%async_computation | async-start | bytes 7077888 | tf_op jit(solution)/shard_map/all_to_all | solution.py:94
  367.1 7.3 collective-permute-start.4
  378.1 7.3 collective-permute-start.6
  389.0 7.3 collective-permute-start.8
  399.9 7.3 collective-permute-start.10
  410.9 7.3 collective-permute-start.12
  421.8 7.3 collective-permute-start.14
  454.6 7.8 collective-permute-start.20
  571.9 7.3 collective-permute-start.44
  580.8 7.3 collective-permute-start.46
  607.6 7.3 collective-permute-start.52
  616.5 7.3 collective-permute-start.54
  634.4 7.3 collective-permute-start.58
  643.3 7.5 collective-permute-start.60
  652.2 7.3 collective-permute-start.62
  661.1 7.3 collective-permute-start.64
  856.3 7.3 collective-permute-start.88
  865.3 7.3 collective-permute-start.90
  874.2 7.3 collective-permute-start.92
  883.1 7.3 collective-permute-start.94
  892.0 7.5 collective-permute-start.96
  936.6 7.4 collective-permute-start.106
  1152.9 7.5 collective-permute-start.132
  1233.3 7.4 collective-permute-start.150
  (163 other events, 6784.1 us)
where the time goes:
time: 1330 us; the launch traced here: 1310 us
  starting transfers between devices  543 us (41%)
  blocking collectives  262 us (20%)
  other arithmetic  236 us (18%)
  local copies, waits for them, and re-layouts  166 us (12%)
  waiting for transfers between devices  90.9 us (7%)
    ppermute x77, starting transfers between devices, padded_2(): lax.ppermute(tail, axis, [(i, (i + 1) % count) for i in range(ends)])  439 us
    reduce_sum x1, other arithmetic, on_device(): forcing = weights * jnp.mean(blocks, axis=(3, 5))  155 us
    psum x3, blocking collectives, level_squares(): return lax.psum(jnp.sum(residual * residual), ('space', 'tm'))  128 us
    convert_element_type x1, local copies, waits for them, and re-layouts, on_device(): innovations.reshape(step_dev, levels, fine_rows // 4, 4, fine_cols // 4, 4)  115 us
    ppermute x77, starting transfers between devices, padded_2(): lax.ppermute(head, axis, [((i + 1) % count, i) for i in range(ends)])  99.5 us
    ppermute x77, waiting for transfers between devices, padded_2(): lax.ppermute(tail, axis, [(i, (i + 1) % count) for i in range(ends)])  90.7 us
    psum x2, blocking collectives, level_curve(): return lax.psum(jnp.sum(direction * hessian_image), ('space', 'tm'))  89.1 us
    all_gather x1, blocking collectives, on_device(): lax.all_gather(obs_counts, 'tm', axis=0, tiled=True).astype(jnp.float32)  44.9 us
  transfers between devices with their start and end apart: 155, of which 77 were waited for; matrix products, arithmetic and copies ran while one was open for 1% of the time, Pallas kernels for 0%

commit v1 on v0

--- a/solution.py
+++ b/solution.py
@@ -1,9 +1,610 @@
+import functools
+
 import jax
 import jax.numpy as jnp
 from jax import lax
+from jax.experimental import pallas as pl
+from jax.experimental.pallas import tpu as pltpu
 from jax.sharding import PartitionSpec as P
 
 ITERS = 3
+F32 = jnp.float32
+BF16 = jnp.bfloat16
+MESH = pl.DeviceIdType.MESH
+BLOCK = 4
+COARSE = 4
+
+
+def restrict_kernel(inn, counts, diff, cour, forcing, weights, diff_t, cour_t, summed):
+    levels, fine_rows, fine_cols = inn.shape[1:]
+    rows, cols = fine_rows // COARSE, fine_cols // COARSE
+    weights[0] = counts[0].astype(F32)
+    wide = 128 * COARSE
+    pick = jnp.where(
+        lax.broadcasted_iota(jnp.int32, (wide, 128), 0) // COARSE
+        == lax.broadcasted_iota(jnp.int32, (wide, 128), 1),
+        1.0 / (COARSE * COARSE),
+        0.0,
+    ).astype(BF16)
+    for part in range(cols // 128):
+        block = inn[0, :, :, part * wide : (part + 1) * wide].reshape(levels * fine_rows, wide)
+        summed[part] = jnp.dot(block, pick, preferred_element_type=F32)
+    for row in range(rows):
+        for part in range(cols // 128):
+            total = summed[part, pl.ds(COARSE * row, levels, stride=fine_rows), :]
+            for sub in range(1, COARSE):
+                total += summed[part, pl.ds(COARSE * row + sub, levels, stride=fine_rows), :]
+            at = slice(part * 128, (part + 1) * 128)
+            forcing[0, 0, row, :, at] = total * weights[0, row : row + 1, at]
+
+    @pl.when(pl.program_id(1) == 0)
+    def _():
+        for row in range(rows):
+            diff_t[0, row] = diff[:, row, :]
+            cour_t[0, row] = cour[:, row, :]
+
+
+def restrict_call(innovations, obs_counts, diffusion, courant, sections):
+    steps, levels, fine_rows, fine_cols = innovations.shape
+    part = levels // sections
+    rows, cols = fine_rows // COARSE, fine_cols // COARSE
+    field = pl.BlockSpec((part, rows, cols), lambda g, t: (g, 0, 0))
+    field_t = pl.BlockSpec((1, rows, part, cols), lambda g, t: (g, 0, 0, 0))
+    step = pl.BlockSpec((1, rows, cols), lambda g, t: (t, 0, 0))
+    return pl.pallas_call(
+        restrict_kernel,
+        grid=(sections, steps),
+        in_specs=[
+            pl.BlockSpec((1, part, fine_rows, fine_cols), lambda g, t: (t, g, 0, 0)),
+            step,
+            field,
+            field,
+        ],
+        out_specs=[
+            pl.BlockSpec((1, 1, rows, part, cols), lambda g, t: (g, t, 0, 0, 0)),
+            step,
+            field_t,
+            field_t,
+        ],
+        out_shape=[
+            jax.ShapeDtypeStruct((sections, steps, rows, part, cols), F32),
+            jax.ShapeDtypeStruct((steps, rows, cols), F32),
+            jax.ShapeDtypeStruct((sections, rows, part, cols), F32),
+            jax.ShapeDtypeStruct((sections, rows, part, cols), F32),
+        ],
+        scratch_shapes=[pltpu.VMEM((cols // 128, part * fine_rows, 128), F32)],
+        compiler_params=pltpu.CompilerParams(vmem_limit_bytes=48 * 2**20),
+        name="restrict",
+    )(innovations, obs_counts, diffusion, courant)
+
+
+def expand_kernel(control, residual, increment, residual_out, held, repeated):
+    rows, cols = residual_out.shape[1:]
+    part = control.shape[0] // rows
+    level = pl.program_id(0)
+    wide = 128 * COARSE
+
+    @pl.when(level == 0)
+    def _():
+        for piece in range(cols // 128):
+            held[0, piece] = control[:, piece * 128 : (piece + 1) * 128]
+            held[1, piece] = residual[:, piece * 128 : (piece + 1) * 128]
+
+    pick = jnp.where(
+        lax.broadcasted_iota(jnp.int32, (128, wide), 1) // COARSE
+        == lax.broadcasted_iota(jnp.int32, (128, wide), 0),
+        1.0,
+        0.0,
+    ).astype(BF16)
+    for piece in range(cols // 128):
+        at = pl.ds(level, rows, stride=part)
+        residual_out[0, :, piece * 128 : (piece + 1) * 128] = held[1, piece, at, :]
+        values = held[0, piece, at, :]
+        for sub in range(COARSE):
+            repeated[piece, pl.ds(sub, rows, stride=COARSE), :] = values
+        rest = repeated[piece]
+        total = None
+        for _ in range(3):
+            head = rest.astype(BF16)
+            rest = rest - head.astype(F32)
+            spread = jnp.dot(head, pick, preferred_element_type=F32)
+            total = spread if total is None else total + spread
+        increment[0, :, piece * wide : (piece + 1) * wide] = total
+
+
+def expand_call(control, residual):
+    rows, part, cols = control.shape
+    whole = pl.BlockSpec((rows * part, cols), lambda l: (0, 0))
+    return pl.pallas_call(
+        expand_kernel,
+        grid=(part,),
+        in_specs=[whole, whole],
+        out_specs=[
+            pl.BlockSpec((1, rows * COARSE, cols * COARSE), lambda l: (l, 0, 0)),
+            pl.BlockSpec((1, rows, cols), lambda l: (l, 0, 0)),
+        ],
+        out_shape=[
+            jax.ShapeDtypeStruct((part, rows * COARSE, cols * COARSE), F32),
+            jax.ShapeDtypeStruct((part, rows, cols), F32),
+        ],
+        scratch_shapes=[
+            pltpu.VMEM((2, cols // 128, rows * part, 128), F32),
+            pltpu.VMEM((cols // 128, rows * COARSE, 128), F32),
+        ],
+        compiler_params=pltpu.CompilerParams(vmem_limit_bytes=32 * 2**20),
+        name="expand",
+    )(control.reshape(rows * part, cols), residual.reshape(rows * part, cols))
+
+
+def solve_kernel(
+    n_space,
+    n_tm,
+    forcing,
+    weights,
+    diff,
+    cour,
+    control,
+    residual,
+    co_a,
+    co_b,
+    co_d,
+    states,
+    wts,
+    lam,
+    direction,
+    p_send,
+    p_recv,
+    w_recv,
+    edge_recv,
+    halo_recv,
+    send_buf,
+    swap_recv,
+    red_src,
+    red_tm,
+    red_space,
+    p_sems,
+    w_sems,
+    edge_sems,
+    halo_sems,
+    swap_sems,
+    red_tm_sems,
+    red_space_sems,
+):
+    steps, rows, part, cols = forcing.shape[1:]
+    total_steps = steps * n_tm
+    halo = total_steps - 1
+    pad = halo + 1
+    place = lax.axis_index("space")
+    section = lax.axis_index("tm")
+    above, below = place - 1, place + 1
+    has_above, has_below = place > 0, place < n_space - 1
+    own = pl.ds(pad, rows)
+    top, bottom = pl.ds(pad - halo, halo), pl.ds(pad + rows, halo)
+
+    def over_rows(low, count, fn):
+        blocks = (count + BLOCK - 1) // BLOCK
+
+        def one(block, carry):
+            fn(low + block * BLOCK)
+            return carry
+
+        lax.fori_loop(0, blocks, one, 0)
+
+    def clear(ref, count):
+        def one(row, carry):
+            ref[row] = jnp.zeros(ref.shape[1:], F32)
+            return carry
+
+        lax.fori_loop(0, count, one, 0)
+
+    def to(axis, peer):
+        return {"device_id": {axis: peer}, "device_id_type": MESH}
+
+    edge_recv[...] = jnp.zeros_like(edge_recv)
+    for side in range(2):
+        for k in range(2):
+            clear(halo_recv.at[side, k], halo)
+        for k in range(swap_recv.shape[0]):
+            clear(swap_recv.at[k, side], halo)
+
+    tm_peers = [lax.rem(section + k, n_tm) for k in range(1, n_tm)]
+    space_peers = [lax.rem(place + k, n_space) for k in range(1, n_space)]
+    barrier = pltpu.get_barrier_semaphore()
+    for peer in tm_peers:
+        pl.semaphore_signal(barrier, inc=1, **to("tm", peer))
+    for peer in space_peers:
+        pl.semaphore_signal(barrier, inc=1, **to("space", peer))
+    pl.semaphore_wait(barrier, n_tm - 1 + n_space - 1)
+
+    def pair(up_src, down_src, up_dst, down_dst, sems):
+        up = pltpu.make_async_remote_copy(
+            src_ref=up_src, dst_ref=up_dst, send_sem=sems.at[0, 0], recv_sem=sems.at[1, 0], **to("space", above)
+        )
+        down = pltpu.make_async_remote_copy(
+            src_ref=down_src, dst_ref=down_dst, send_sem=sems.at[0, 1], recv_sem=sems.at[1, 1], **to("space", below)
+        )
+        return [(has_above, has_below, up), (has_below, has_above, down)]
+
+    def start(copies):
+        for sends, _, copy in copies:
+            pl.when(sends)(copy.start)
+
+    def finish(copies):
+        for sends, receives, copy in copies:
+            pl.when(sends)(copy.wait_send)
+            pl.when(receives)(copy.wait_recv)
+
+    edge_copies = []
+    for k, field in enumerate((diff, cour)):
+        edge_copies += pair(
+            field.at[:, pl.ds(0, 1)],
+            field.at[:, pl.ds(rows - 1, 1)],
+            edge_recv.at[1, k],
+            edge_recv.at[0, k],
+            edge_sems.at[k],
+        )
+    start(edge_copies)
+    w_copies = []
+    for k, peer in enumerate(tm_peers):
+        w_copies.append(
+            pltpu.make_async_remote_copy(
+                src_ref=weights,
+                dst_ref=w_recv.at[section],
+                send_sem=w_sems.at[0, k],
+                recv_sem=w_sems.at[1, section],
+                **to("tm", peer),
+            )
+        )
+    for copy in w_copies:
+        copy.start()
+    halo_copies = []
+    for k, field in enumerate((diff, cour)):
+        halo_copies += pair(
+            field.at[section, pl.ds(0, halo)],
+            field.at[section, pl.ds(rows - halo, halo)],
+            halo_recv.at[1, k],
+            halo_recv.at[0, k],
+            halo_sems.at[k],
+        )
+    start(halo_copies)
+
+    clear(co_a, co_a.shape[0])
+    clear(co_b, co_b.shape[0])
+    clear(co_d, co_d.shape[0])
+
+    def put_coefs(row, d, c, inside=None):
+        a = 1.0 - 4.0 * d - c
+        b = d + c
+        if inside is not None:
+            a = jnp.where(inside, a, 0.0)
+        co_a[row] = a
+        co_b[row] = b
+        co_d[row] = d
+
+    def adjoint_block(slot, low):
+        here = pl.ds(low, BLOCK)
+        around = pl.ds(low - 1, BLOCK + 2)
+        y = lam[slot, around]
+        s = co_d[around] * y
+        yc, sc = y[1:-1], s[1:-1]
+        return (
+            co_a[here] * yc
+            + (s[:-2] + s[2:])
+            + pltpu.roll(sc, 1, 2)
+            + pltpu.roll(co_b[here] * yc, cols - 1, 2)
+        )
+
+    def adjoint_step(slot, grown):
+        def fn(low):
+            lam[1 - slot, pl.ds(low, BLOCK)] = adjoint_block(slot, low)
+
+        over_rows(pad - grown, rows + 2 * grown, fn)
+
+    def add_rows(slot, at, term, count):
+        def fn(row, carry):
+            lam[slot, at + row] = lam[slot, at + row] + term[row]
+            return carry
+
+        lax.fori_loop(0, count, fn, 0)
+
+    def clear_lam():
+        clear(lam.at[0], lam.shape[1])
+        clear(lam.at[1], lam.shape[1])
+
+    finish(edge_copies)
+    reach = steps - 1
+    p_copies = []
+    for turn in range(n_tm):
+        group = lax.rem(section + turn + 1, n_tm)
+
+        def fill(row, carry, group=group):
+            put_coefs(pad + row, diff[group, row], cour[group, row])
+            return carry
+
+        lax.fori_loop(0, rows, fill, 0)
+        put_coefs(pad - 1, edge_recv[0, 0, group, 0], edge_recv[0, 1, group, 0], has_above)
+        put_coefs(pad + rows, edge_recv[1, 0, group, 0], edge_recv[1, 1, group, 0], has_below)
+        clear_lam()
+        slot = 0
+        add_rows(slot, pad, forcing.at[group, steps - 1], rows)
+        for k in range(1, steps):
+            adjoint_step(slot, k)
+            slot = 1 - slot
+            add_rows(slot, pad, forcing.at[group, steps - 1 - k], rows)
+        target = p_send.at[turn] if turn < n_tm - 1 else p_recv.at[section]
+
+        def keep(row, carry, slot=slot, target=target):
+            target[row] = lam[slot, pad - reach + row]
+            return carry
+
+        lax.fori_loop(0, rows + 2 * reach, keep, 0)
+        if turn < n_tm - 1:
+            copy = pltpu.make_async_remote_copy(
+                src_ref=p_send.at[turn],
+                dst_ref=p_recv.at[section],
+                send_sem=p_sems.at[0, turn],
+                recv_sem=p_sems.at[1, section],
+                **to("tm", group),
+            )
+            copy.start()
+            p_copies.append(copy)
+
+    for t in range(total_steps):
+        clear(states.at[t], states.shape[1])
+        clear(wts.at[t], wts.shape[1])
+
+    def from_peer(k, ref_src, ref_dst, sems):
+        peer = tm_peers[k]
+        return pltpu.make_async_remote_copy(
+            src_ref=ref_src, dst_ref=ref_dst.at[peer], send_sem=sems.at[0, k], recv_sem=sems.at[1, peer], **to("tm", peer)
+        )
+
+    for k in range(n_tm - 1):
+        w_copies[k].wait_send()
+        from_peer(k, weights, w_recv, w_sems).wait_recv()
+    w_recv[section] = weights[...]
+
+    def spread_weights(row, carry):
+        for t in range(total_steps):
+            line = w_recv[t // steps, t % steps, pl.ds(row, 1), :]
+            wts[t, pad + row] = jnp.broadcast_to(line, (part, cols))
+        return carry
+
+    lax.fori_loop(0, rows, spread_weights, 0)
+
+    finish(halo_copies)
+
+    def fill_halo(row, carry):
+        put_coefs(pad - halo + row, halo_recv[0, 0, row], halo_recv[0, 1, row], has_above)
+        put_coefs(pad + rows + row, halo_recv[1, 0, row], halo_recv[1, 1, row], has_below)
+        return carry
+
+    lax.fori_loop(0, halo, fill_halo, 0)
+
+    for k in range(n_tm - 1):
+        p_copies[k].wait_send()
+        from_peer(k, p_send.at[k], p_recv, p_sems).wait_recv()
+    clear_lam()
+    slot = 0
+    grown = reach
+    add_rows(slot, pad - reach, p_recv.at[n_tm - 1], rows + 2 * reach)
+    for other in range(n_tm - 2, -1, -1):
+        for _ in range(steps):
+            grown += 1
+            adjoint_step(slot, grown)
+            slot = 1 - slot
+        add_rows(slot, pad - reach, p_recv.at[other], rows + 2 * reach)
+
+    def scatter(slot, k):
+        copies = pair(lam.at[slot, top], lam.at[slot, bottom], swap_recv.at[k, 1], swap_recv.at[k, 0], swap_sems.at[k])
+        start(copies)
+        return copies
+
+    def add_scattered(slot, k):
+        add_rows(slot, pad, swap_recv.at[k, 0], halo)
+        add_rows(slot, pad + rows - halo, swap_recv.at[k, 1], halo)
+
+    def gather(k):
+        copies = pair(
+            residual.at[pl.ds(0, halo)],
+            residual.at[pl.ds(rows - halo, halo)],
+            swap_recv.at[k, 1],
+            swap_recv.at[k, 0],
+            swap_sems.at[k],
+        )
+        start(copies)
+        return copies
+
+    def reduce_over(axis, me, peers, count, tile, k, src, slots, sems):
+        src[...] = tile
+        slots[me] = tile
+        copies = []
+        for j, peer in enumerate(peers):
+            copies.append(
+                pltpu.make_async_remote_copy(
+                    src_ref=src,
+                    dst_ref=slots.at[me],
+                    send_sem=sems.at[0, j],
+                    recv_sem=sems.at[1, me],
+                    **to(axis, peer),
+                )
+            )
+        for copy in copies:
+            copy.start()
+        for j, peer in enumerate(peers):
+            copies[j].wait_send()
+            pltpu.make_async_remote_copy(
+                src_ref=src,
+                dst_ref=slots.at[peer],
+                send_sem=sems.at[0, j],
+                recv_sem=sems.at[1, peer],
+                **to(axis, peer),
+            ).wait_recv()
+        total = slots[0]
+        for j in range(1, count):
+            total = total + slots[j]
+        return total
+
+    def reduce_all(partial, k):
+        tile = partial[:, :128]
+        for piece in range(1, cols // 128):
+            tile = tile + partial[:, piece * 128 : (piece + 1) * 128]
+        tile = reduce_over("tm", section, tm_peers, n_tm, tile, k, red_src.at[k, 0], red_tm.at[k], red_tm_sems.at[k])
+        tile = reduce_over(
+            "space", place, space_peers, n_space, tile, k, red_src.at[k, 1], red_space.at[k], red_space_sems.at[k]
+        )
+        return jnp.sum(jnp.sum(tile, axis=0, keepdims=True), axis=1, keepdims=True)
+
+    none = jnp.zeros((part, cols), F32)
+    copies = scatter(slot, 0)
+    finish(copies)
+    add_scattered(slot, 0)
+
+    def take_rhs(row, acc, slot=slot):
+        value = lam[slot, pad + row]
+        residual[row] = value
+        control[row] = jnp.zeros_like(value)
+        return acc + value * value
+
+    partial = lax.fori_loop(0, rows, take_rhs, none)
+    swap = 1
+    red = 0
+    norm_now = None
+    for iter_no in range(ITERS):
+        copies = gather(swap)
+        norm_next = reduce_all(partial, red)
+        red += 1
+        finish(copies)
+        first = iter_no == 0
+        beta = None if first else norm_next / norm_now
+        norm_now = norm_next
+
+        def new_direction(row, value, beta=beta):
+            if beta is not None:
+                value = value + beta * direction[row]
+            direction[row] = value
+            states[0, row] = value
+            return value
+
+        def own_direction(row, acc, new=new_direction):
+            value = new(pad + row, residual[row])
+            return acc + value * value
+
+        def halo_direction(row, carry, new=new_direction, swap=swap):
+            new(pad - halo + row, swap_recv[swap, 0, row])
+            new(pad + rows + row, swap_recv[swap, 1, row])
+            return carry
+
+        squares = lax.fori_loop(0, rows, own_direction, none)
+        lax.fori_loop(0, halo, halo_direction, 0)
+        swap += 1
+        clear_lam()
+
+        def forward_step(t, carry):
+            def fn(low):
+                here = pl.ds(low, BLOCK)
+                x = states[t - 1, pl.ds(low - 1, BLOCK + 2)]
+                xc = x[1:-1]
+                states[t, here] = (
+                    co_a[here] * xc
+                    + co_d[here] * (x[:-2] + x[2:] + pltpu.roll(xc, cols - 1, 2))
+                    + co_b[here] * pltpu.roll(xc, 1, 2)
+                )
+
+            over_rows(pad - halo + t, rows + 2 * (halo - t), fn)
+            return carry
+
+        lax.fori_loop(1, total_steps, forward_step, 0)
+
+        def last_term(row, acc):
+            x = states[total_steps - 1, pad + row]
+            g = wts[total_steps - 1, pad + row] * x
+            lam[0, pad + row] = g
+            return acc + g * x
+
+        squares = lax.fori_loop(0, rows, last_term, squares)
+
+        def backward_step(k, acc):
+            t = total_steps - 2 - k
+            slot = lax.rem(k, 2)
+            grown = halo - t
+
+            def one(block, acc):
+                low = pad - grown + block * BLOCK
+                here = pl.ds(low, BLOCK)
+                x = states[t, here]
+                g = wts[t, here] * x
+                lam[1 - slot, here] = adjoint_block(slot, low) + g
+                return acc + jnp.sum(g * x, axis=0)
+
+            return lax.fori_loop(0, (rows + 2 * grown + BLOCK - 1) // BLOCK, one, acc)
+
+        squares = lax.fori_loop(0, total_steps - 1, backward_step, squares)
+        slot = (total_steps - 1) % 2
+        copies = scatter(slot, swap)
+        step_len = norm_now / reduce_all(squares, red)
+        red += 1
+        finish(copies)
+        add_scattered(slot, swap)
+        swap += 1
+
+        def update(row, acc, slot=slot, step_len=step_len):
+            d = direction[pad + row]
+            control[row] = control[row] + step_len * d
+            value = residual[row] - step_len * (d + lam[slot, pad + row])
+            residual[row] = value
+            return acc + value * value
+
+        partial = lax.fori_loop(0, rows, update, none)
+
+
+def solve_call(forcing, weights, diff_t, cour_t, n_space, n_tm):
+    sections, steps, rows, part, cols = forcing.shape
+    total_steps = steps * n_tm
+    halo = total_steps - 1
+    ext = rows + 2 * (halo + 1) + BLOCK
+    p_rows = rows + 2 * (steps - 1)
+    swaps = 1 + 2 * ITERS
+    reds = 2 * ITERS
+    vmem = pl.BlockSpec(memory_space=pltpu.VMEM)
+    row = (part, cols)
+    dma = pltpu.SemaphoreType.DMA
+    return pl.pallas_call(
+        functools.partial(solve_kernel, n_space, n_tm),
+        out_shape=[jax.ShapeDtypeStruct((rows, *row), F32)] * 2,
+        in_specs=[vmem] * 4,
+        out_specs=[vmem] * 2,
+        scratch_shapes=[
+            pltpu.VMEM((ext, *row), F32),
+            pltpu.VMEM((ext, *row), F32),
+            pltpu.VMEM((ext, *row), F32),
+            pltpu.VMEM((total_steps, ext, *row), F32),
+            pltpu.VMEM((total_steps, ext, *row), F32),
+            pltpu.VMEM((2, ext, *row), F32),
+            pltpu.VMEM((ext, *row), F32),
+            pltpu.VMEM((n_tm - 1, p_rows, *row), F32),
+            pltpu.VMEM((n_tm, p_rows, *row), F32),
+            pltpu.VMEM((n_tm, steps, rows, cols), F32),
+            pltpu.VMEM((2, 2, n_tm, 1, *row), F32),
+            pltpu.VMEM((2, 2, halo, *row), F32),
+            pltpu.VMEM((1, 8, 128), F32),
+            pltpu.VMEM((swaps, 2, halo, *row), F32),
+            pltpu.VMEM((reds, 2, part, 128), F32),
+            pltpu.VMEM((reds, n_tm, part, 128), F32),
+            pltpu.VMEM((reds, n_space, part, 128), F32),
+            dma((2, n_tm)),
+            dma((2, n_tm)),
+            dma((2, 2, 2)),
+            dma((2, 2, 2)),
+            dma((swaps, 2, 2)),
+            dma((reds, 2, n_tm)),
+            dma((reds, 2, n_space)),
+        ],
+        compiler_params=pltpu.CompilerParams(
+            collective_id=0, has_side_effects=True, vmem_limit_bytes=60 * 2**20
+        ),
+        name="solve",
+    )(forcing, weights, diff_t, cour_t)
 
 
 def padded_2(cells, sides, width):
@@ -86,6 +687,11 @@
         innovations.shape[3],
     )
     lev_part = levels // n_sections
+    rows, cols = fine_rows // COARSE, fine_cols // COARSE
+    if lev_part == 8 and rows % 8 == 0 and rows >= total_steps - 1 and cols % 128 == 0:
+        forced = restrict_call(innovations, obs_counts, diffusion, courant, n_sections)
+        solved = solve_call(*forced, lax.axis_size("space"), n_sections)
+        return tuple(expand_call(*solved))
     blocks = innovations.reshape(step_dev, levels, fine_rows // 4, 4, fine_cols // 4, 4).astype(
         jnp.float32
     )

time: 1330 us -> 203 us (0.15); the launches traced: 1310 us -> 202 us
  starting transfers between devices: 543 us -> 0 us
  blocking collectives: 262 us -> 0 us
  other arithmetic: 236 us -> 0 us
  Pallas kernels: 0 us -> 194 us
  local copies, waits for them, and re-layouts: 166 us -> 8.05 us
  waiting for transfers between devices: 90.9 us -> 0 us
    ppermute x154 -> x0, starting transfers between devices: 538 us -> none  [the longest x77 439 us: padded_2(): lax.ppermute(tail, axis, [(i, (i + 1) % count) for i in range(ends)])]
    psum x5 -> x0, blocking collectives: 217 us -> none  [the longest x3 128 us: level_squares(): return lax.psum(jnp.sum(residual * residual), ('space', 'tm'))]
    pallas_call x0 -> x3, Pallas kernels: none -> 194 us  [the longest x1 165 us: solve_call(): pl.pallas_call(functools.partial(solve_kernel, n_space, n_tm), out_shape=...]
    reduce_sum x6 -> x0, other arithmetic: 161 us -> none  [the longest x1 155 us: on_device(): forcing = weights * jnp.mean(blocks, axis=(3, 5))]
    convert_element_type x1 -> x0, local copies, waits for them, and re-layouts: 115 us -> none  [on_device(): innovations.reshape(step_dev, levels, fine_rows // 4, 4, fine_cols // 4, 4)]
    ppermute x154 -> x0, waiting for transfers between devices: 90.9 us -> none  [the longest x77 90.7 us: padded_2(): lax.ppermute(tail, axis, [(i, (i + 1) % count) for i in range(ends)])]
    mul x89 -> x0, other arithmetic: 45.6 us -> none  [the longest x44 21.6 us: adjoint(): spread = diffusion * state_field]
    all_gather x1 -> x0, blocking collectives: 44.9 us -> none  [on_device(): lax.all_gather(obs_counts, 'tm', axis=0, tiled=True).astype(jnp.float32)]
  transfers between devices with their start and end apart: 155 -> 0, of which waited for: 77 -> 0; matrix products, arithmetic and copies ran while one was open for 1% -> 0% of each run, Pallas kernels for 0% -> 0%
where the time goes in v1:
time: 203 us; the launch traced here: 202 us
  Pallas kernels  194 us (96%)
  local copies, waits for them, and re-layouts  8.05 us (4%)
    pallas_call x1, Pallas kernels, solve_call(): pl.pallas_call(functools.partial(solve_kernel, n_space, n_tm), out_shape=...  165 us
    pallas_call x1, Pallas kernels, restrict_call(): pl.pallas_call(restrict_kernel, grid=(sections, steps), in_specs=[pl.Bloc...  23.1 us
    unnamed x16, local copies, waits for them, and re-layouts  8.05 us
    pallas_call x1, Pallas kernels, expand_call(): pl.pallas_call(expand_kernel, grid=(part,), in_specs=[whole, whole], out_...  5.3 us

profile of v1, /device:TPU:0, one launch (start us, length us, event | category | flops | bytes accessed | tf_op | source)
XLA Modules:
  0.0 202.4 jit_solution(12576525517764338391)
XLA Ops:
  0.6 0.0 copy-start
  0.6 1.3 copy-done
  1.9 0.0 copy-start.1
  1.9 1.3 copy-done.1
  3.2 0.0 copy-start.6
  3.2 0.9 copy-done.6
  4.1 23.1 %restrict.1 = (f32[4,3,24,8,384]{4,3,2,1,0:T(8,128)}, f32[3,24,384]{2,1,0:T(8,128)S(1)}, f32[4,24,8,384]{3,2,1,0:T(8,128)S(1)}, f32[4,24,8,384]{3,2,1,0:T(8,128)S(1)}) custom-call(bf16[3,32,96,1536]{3,2,1,0:T(8,128)(2,1)} %inn.1, s32[3,24,384]{2,1,0:T(8,128)S(1)} %copy-done.6, f32[32,24,384]{2,1,0:T(8,128)S(1)} %copy-done, f32[32,24,384]{2,1,0:T(8,128)S(1)} %copy-done.1), custom_call_target="tpu_custom_call" | custom-call | tf_op jit(solution)/shard_map/restrict/pallas_call | solution.py:54
  27.2 0.0 copy-start.2
  27.2 1.0 copy-done.2
  28.2 0.0 copy-start.3
  28.2 1.0 copy-done.3
  29.2 0.0 copy-start.7
  29.2 0.6 copy-done.7
  29.9 165.3 %solve.1 = (f32[24,8,384]{2,1,0:T(8,128)}, f32[24,8,384]{2,1,0:T(8,128)}) custom-call(f32[4,3,24,8,384]{4,3,2,1,0:T(8,128)} %get-tuple-element.8.forcing, f32[3,24,384]{2,1,0:T(8,128)} %copy-done.7, f32[4,24,8,384]{3,2,1,0:T(8,128)} %copy-done.2, f32[4,24,8,384]{3,2,1,0:T(8,128)} %copy-done.3), custom_call_target="tpu_custom_call" | custom-call | tf_op jit(solution)/shard_map/solve/pallas_call | solution.py:572
  195.2 0.0 copy-start.4
  195.2 1.0 copy-done.4
  196.1 0.0 copy-start.5
  196.1 1.0 copy-done.5
  197.1 5.3 %expand.1 = (f32[8,96,1536]{2,1,0:T(8,128)}, f32[8,24,384]{2,1,0:T(8,128)}) custom-call(f32[192,384]{1,0:T(8,128)S(1)} %bitcast.2, f32[192,384]{1,0:T(8,128)S(1)} %bitcast.3), custom_call_target="tpu_custom_call" | custom-call | tf_op jit(solution)/shard_map/expand/pallas_call | solution.py:118
Async XLA Ops:
  0.6 1.3 copy-start
  1.9 1.3 copy-start.1
  3.2 0.9 copy-start.6
  27.2 1.0 copy-start.2
  28.2 1.0 copy-start.3
  29.2 0.6 copy-start.7
  195.2 1.0 copy-start.4
  196.1 1.0 copy-start.5

commit v2 on v1

--- a/solution.py
+++ b/solution.py
@@ -12,10 +12,11 @@
 BF16 = jnp.bfloat16
 MESH = pl.DeviceIdType.MESH
 BLOCK = 4
+ROWS = 4
 COARSE = 4
 
 
-def restrict_kernel(inn, counts, diff, cour, forcing, weights, diff_t, cour_t, summed):
+def restrict_kernel(inn, counts, diff, cour, forcing, weights, diff_t, cour_t, summed, turned):
     levels, fine_rows, fine_cols = inn.shape[1:]
     rows, cols = fine_rows // COARSE, fine_cols // COARSE
     weights[0] = counts[0].astype(F32)
@@ -29,13 +30,15 @@
     for part in range(cols // 128):
         block = inn[0, :, :, part * wide : (part + 1) * wide].reshape(levels * fine_rows, wide)
         summed[part] = jnp.dot(block, pick, preferred_element_type=F32)
-    for row in range(rows):
-        for part in range(cols // 128):
-            total = summed[part, pl.ds(COARSE * row, levels, stride=fine_rows), :]
+    for part in range(cols // 128):
+        at = slice(part * 128, (part + 1) * 128)
+        scale = weights[0, :, at]
+        for level in range(levels):
+            total = summed[part, pl.ds(level * fine_rows, rows, stride=COARSE), :]
             for sub in range(1, COARSE):
-                total += summed[part, pl.ds(COARSE * row + sub, levels, stride=fine_rows), :]
-            at = slice(part * 128, (part + 1) * 128)
-            forcing[0, 0, row, :, at] = total * weights[0, row : row + 1, at]
+                total += summed[part, pl.ds(level * fine_rows + sub, rows, stride=COARSE), :]
+            turned[part, pl.ds(level, rows, stride=levels), :] = total * scale
+        forcing[0, 0, :, :, at] = turned[part].reshape(rows, levels, 128)
 
     @pl.when(pl.program_id(1) == 0)
     def _():
@@ -72,7 +75,10 @@
             jax.ShapeDtypeStruct((sections, rows, part, cols), F32),
             jax.ShapeDtypeStruct((sections, rows, part, cols), F32),
         ],
-        scratch_shapes=[pltpu.VMEM((cols // 128, part * fine_rows, 128), F32)],
+        scratch_shapes=[
+            pltpu.VMEM((cols // 128, part * fine_rows, 128), F32),
+            pltpu.VMEM((cols // 128, part * rows, 128), F32),
+        ],
         compiler_params=pltpu.CompilerParams(vmem_limit_bytes=48 * 2**20),
         name="restrict",
     )(innovations, obs_counts, diffusion, courant)
@@ -190,12 +196,24 @@
 
         lax.fori_loop(0, blocks, one, 0)
 
-    def clear(ref, count):
-        def one(row, carry):
-            ref[row] = jnp.zeros(ref.shape[1:], F32)
+    def by_block(count, fn, carry=0):
+        full = count // ROWS
+
+        def one(block, carry):
+            return fn(block * ROWS, ROWS, carry)
+
+        if full:
+            carry = lax.fori_loop(0, full, one, carry)
+        if count % ROWS:
+            carry = fn(full * ROWS, count % ROWS, carry)
+        return carry
+
+    def clear(ref, count, first=0):
+        def one(row, size, carry):
+            ref[pl.ds(first + row, size)] = jnp.zeros((size, *ref.shape[1:]), F32)
             return carry
 
-        lax.fori_loop(0, count, one, 0)
+        by_block(count, one)
 
     def to(axis, peer):
         return {"device_id": {axis: peer}, "device_id_type": MESH}
@@ -301,11 +319,12 @@
         over_rows(pad - grown, rows + 2 * grown, fn)
 
     def add_rows(slot, at, term, count):
-        def fn(row, carry):
-            lam[slot, at + row] = lam[slot, at + row] + term[row]
+        def fn(row, size, carry):
+            here = pl.ds(at + row, size)
+            lam[slot, here] = lam[slot, here] + term[pl.ds(row, size)]
             return carry
 
-        lax.fori_loop(0, count, fn, 0)
+        by_block(count, fn)
 
     def clear_lam():
         clear(lam.at[0], lam.shape[1])
@@ -317,11 +336,12 @@
     for turn in range(n_tm):
         group = lax.rem(section + turn + 1, n_tm)
 
-        def fill(row, carry, group=group):
-            put_coefs(pad + row, diff[group, row], cour[group, row])
+        def fill(row, size, carry, group=group):
+            here = pl.ds(row, size)
+            put_coefs(pl.ds(pad + row, size), diff[group, here], cour[group, here])
             return carry
 
-        lax.fori_loop(0, rows, fill, 0)
+        by_block(rows, fill)
         put_coefs(pad - 1, edge_recv[0, 0, group, 0], edge_recv[0, 1, group, 0], has_above)
         put_coefs(pad + rows, edge_recv[1, 0, group, 0], edge_recv[1, 1, group, 0], has_below)
         clear_lam()
@@ -333,11 +353,11 @@
             add_rows(slot, pad, forcing.at[group, steps - 1 - k], rows)
         target = p_send.at[turn] if turn < n_tm - 1 else p_recv.at[section]
 
-        def keep(row, carry, slot=slot, target=target):
-            target[row] = lam[slot, pad - reach + row]
+        def keep(row, size, carry, slot=slot, target=target):
+            target[pl.ds(row, size)] = lam[slot, pl.ds(pad - reach + row, size)]
             return carry
 
-        lax.fori_loop(0, rows + 2 * reach, keep, 0)
+        by_block(rows + 2 * reach, keep)
         if turn < n_tm - 1:
             copy = pltpu.make_async_remote_copy(
                 src_ref=p_send.at[turn],
@@ -350,8 +370,9 @@
             p_copies.append(copy)
 
     for t in range(total_steps):
-        clear(states.at[t], states.shape[1])
-        clear(wts.at[t], wts.shape[1])
+        clear(states.at[t], states.shape[1] - pad - rows, pad + rows)
+        clear(wts.at[t], pad)
+        clear(wts.at[t], wts.shape[1] - pad - rows, pad + rows)
 
     def from_peer(k, ref_src, ref_dst, sems):
         peer = tm_peers[k]
@@ -374,12 +395,13 @@
 
     finish(halo_copies)
 
-    def fill_halo(row, carry):
-        put_coefs(pad - halo + row, halo_recv[0, 0, row], halo_recv[0, 1, row], has_above)
-        put_coefs(pad + rows + row, halo_recv[1, 0, row], halo_recv[1, 1, row], has_below)
+    def fill_halo(row, size, carry):
+        here = pl.ds(row, size)
+        put_coefs(pl.ds(pad - halo + row, size), halo_recv[0, 0, here], halo_recv[0, 1, here], has_above)
+        put_coefs(pl.ds(pad + rows + row, size), halo_recv[1, 0, here], halo_recv[1, 1, here], has_below)
         return carry
 
-    lax.fori_loop(0, halo, fill_halo, 0)
+    by_block(halo, fill_halo)
 
     for k in range(n_tm - 1):
         p_copies[k].wait_send()
@@ -460,13 +482,13 @@
     finish(copies)
     add_scattered(slot, 0)
 
-    def take_rhs(row, acc, slot=slot):
-        value = lam[slot, pad + row]
-        residual[row] = value
-        control[row] = jnp.zeros_like(value)
-        return acc + value * value
-
-    partial = lax.fori_loop(0, rows, take_rhs, none)
+    def take_rhs(row, size, acc, slot=slot):
+        value = lam[slot, pl.ds(pad + row, size)]
+        residual[pl.ds(row, size)] = value
+        control[pl.ds(row, size)] = jnp.zeros_like(value)
+        return acc + jnp.sum(value * value, axis=0)
+
+    partial = by_block(rows, take_rhs, none)
     swap = 1
     red = 0
     norm_now = None
@@ -479,24 +501,25 @@
         beta = None if first else norm_next / norm_now
         norm_now = norm_next
 
-        def new_direction(row, value, beta=beta):
+        def new_direction(here, value, beta=beta):
             if beta is not None:
-                value = value + beta * direction[row]
-            direction[row] = value
-            states[0, row] = value
+                value = value + beta.reshape(1, 1, 1) * direction[here]
+            direction[here] = value
+            states[0, here] = value
             return value
 
-        def own_direction(row, acc, new=new_direction):
-            value = new(pad + row, residual[row])
-            return acc + value * value
-
-        def halo_direction(row, carry, new=new_direction, swap=swap):
-            new(pad - halo + row, swap_recv[swap, 0, row])
-            new(pad + rows + row, swap_recv[swap, 1, row])
+        def own_direction(row, size, acc, new=new_direction):
+            value = new(pl.ds(pad + row, size), residual[pl.ds(row, size)])
+            return acc + jnp.sum(value * value, axis=0)
+
+        def halo_direction(row, size, carry, new=new_direction, swap=swap):
+            here = pl.ds(row, size)
+            new(pl.ds(pad - halo + row, size), swap_recv[swap, 0, here])
+            new(pl.ds(pad + rows + row, size), swap_recv[swap, 1, here])
             return carry
 
-        squares = lax.fori_loop(0, rows, own_direction, none)
-        lax.fori_loop(0, halo, halo_direction, 0)
+        squares = by_block(rows, own_direction, none)
+        by_block(halo, halo_direction)
         swap += 1
         clear_lam()
 
@@ -516,13 +539,14 @@
 
         lax.fori_loop(1, total_steps, forward_step, 0)
 
-        def last_term(row, acc):
-            x = states[total_steps - 1, pad + row]
-            g = wts[total_steps - 1, pad + row] * x
-            lam[0, pad + row] = g
-            return acc + g * x
-
-        squares = lax.fori_loop(0, rows, last_term, squares)
+        def last_term(row, size, acc):
+            here = pl.ds(pad + row, size)
+            x = states[total_steps - 1, here]
+            g = wts[total_steps - 1, here] * x
+            lam[0, here] = g
+            return acc + jnp.sum(g * x, axis=0)
+
+        squares = by_block(rows, last_term, squares)
 
         def backward_step(k, acc):
             t = total_steps - 2 - k
@@ -548,14 +572,15 @@
         add_scattered(slot, swap)
         swap += 1
 
-        def update(row, acc, slot=slot, step_len=step_len):
-            d = direction[pad + row]
-            control[row] = control[row] + step_len * d
-            value = residual[row] - step_len * (d + lam[slot, pad + row])
-            residual[row] = value
-            return acc + value * value
-
-        partial = lax.fori_loop(0, rows, update, none)
+        def update(row, size, acc, slot=slot, step_len=step_len.reshape(1, 1, 1)):
+            here, ext = pl.ds(row, size), pl.ds(pad + row, size)
+            d = direction[ext]
+            control[here] = control[here] + step_len * d
+            value = residual[here] - step_len * (d + lam[slot, ext])
+            residual[here] = value
+            return acc + jnp.sum(value * value, axis=0)
+
+        partial = by_block(rows, update, none)
 
 
 def solve_call(forcing, weights, diff_t, cour_t, n_space, n_tm):

time: 203 us -> 193 us (0.951)
  Pallas kernels: 194 us -> 184 us
    pallas_call x1, Pallas kernels: 165 us -> 160 us  [solve_call(): pl.pallas_call(functools.partial(solve_kernel, n_space, n_tm), out_shape=...]
    pallas_call x1, Pallas kernels: 23.1 us -> 18.8 us  [restrict_call(): pl.pallas_call(restrict_kernel, grid=(sections, steps), in_specs=[pl.Bloc...]
where the time goes in v2:
time: 193 us
  Pallas kernels  184 us (95%)
  local copies, waits for them, and re-layouts  8.05 us (4%)
    pallas_call x1, Pallas kernels, solve_call(): pl.pallas_call(functools.partial(solve_kernel, n_space, n_tm), out_shape=...  160 us
    pallas_call x1, Pallas kernels, restrict_call(): pl.pallas_call(restrict_kernel, grid=(sections, steps), in_specs=[pl.Bloc...  18.8 us
    unnamed x16, local copies, waits for them, and re-layouts  8.05 us
    pallas_call x1, Pallas kernels, expand_call(): pl.pallas_call(expand_kernel, grid=(part,), in_specs=[whole, whole], out_...  5.3 us

profile of v2, /device:TPU:0, one launch (start us, length us, event | category | flops | bytes accessed | tf_op | source)
XLA Modules:
  0.0 192.6 jit_solution(17209183870591709324)
XLA Ops:
  0.6 0.0 copy-start
  0.6 1.3 copy-done
  1.9 0.0 copy-start.1
  1.9 1.3 copy-done.1
  3.2 0.0 copy-start.6
  3.2 0.9 copy-done.6
  4.1 18.8 %restrict.1 = (f32[4,3,24,8,384]{4,3,2,1,0:T(8,128)}, f32[3,24,384]{2,1,0:T(8,128)S(1)}, f32[4,24,8,384]{3,2,1,0:T(8,128)S(1)}, f32[4,24,8,384]{3,2,1,0:T(8,128)S(1)}) custom-call(bf16[3,32,96,1536]{3,2,1,0:T(8,128)(2,1)} %inn.1, s32[3,24,384]{2,1,0:T(8,128)S(1)} %copy-done.6, f32[32,24,384]{2,1,0:T(8,128)S(1)} %copy-done, f32[32,24,384]{2,1,0:T(8,128)S(1)} %copy-done.1), custom_call_target="tpu_custom_call" | custom-call | tf_op jit(solution)/shard_map/restrict/pallas_call | solution.py:57
  22.8 0.0 copy-start.2
  22.8 1.0 copy-done.2
  23.9 0.0 copy-start.3
  23.9 1.0 copy-done.3
  24.9 0.0 copy-start.7
  24.9 0.6 copy-done.7
  25.5 159.8 %solve.1 = (f32[24,8,384]{2,1,0:T(8,128)}, f32[24,8,384]{2,1,0:T(8,128)}) custom-call(f32[4,3,24,8,384]{4,3,2,1,0:T(8,128)} %get-tuple-element.8.forcing, f32[3,24,384]{2,1,0:T(8,128)} %copy-done.7, f32[4,24,8,384]{3,2,1,0:T(8,128)} %copy-done.2, f32[4,24,8,384]{3,2,1,0:T(8,128)} %copy-done.3), custom_call_target="tpu_custom_call" | custom-call | tf_op jit(solution)/shard_map/solve/pallas_call | solution.py:597
  185.3 0.0 copy-start.4
  185.3 1.0 copy-done.4
  186.3 0.0 copy-start.5
  186.3 1.0 copy-done.5
  187.3 5.3 %expand.1 = (f32[8,96,1536]{2,1,0:T(8,128)}, f32[8,24,384]{2,1,0:T(8,128)}) custom-call(f32[192,384]{1,0:T(8,128)S(1)} %bitcast.2, f32[192,384]{1,0:T(8,128)S(1)} %bitcast.3), custom_call_target="tpu_custom_call" | custom-call | tf_op jit(solution)/shard_map/expand/pallas_call | solution.py:124
Async XLA Ops:
  0.6 1.3 copy-start
  1.9 1.3 copy-start.1
  3.2 0.9 copy-start.6
  22.8 1.0 copy-start.2
  23.9 1.0 copy-start.3
  24.9 0.6 copy-start.7
  185.3 1.0 copy-start.4
  186.3 1.0 copy-start.5
